TPU v7x, 256 devices: a whole 4x4x8 slice. The times are simulated.
256 devices in a mesh: gx: 4 (over y), gy: 16 (over z, core), gz: 4 (over x).
Axes of the slice: x: 4, y: 4, z: 8, core: 2. Of those that a mesh axis runs over, the one named last changes fastest.
Arguments:
- initial: float32 [256, 512, 1024], P('gx', 'gy', 'gz'), may hold values from -6 to 6
- right_side: float32 [256, 512, 1024], P('gx', 'gy', 'gz'), may hold values from -12 to 12
- shift_field: float32 [256, 512, 1024], P('gx', 'gy', 'gz'), may hold values from 0.5 to 8
Outputs:
- relaxed: float32 [256, 512, 1024], P('gx', 'gy', 'gz')
All inputs are finite; a program needn't handle non-finite values.
Results may differ from a plain program's by a relative error of at most 0.00002.
Values sent between devices are 32-bit elements; how exact they have to be, the bound alone decides.
A program may use at most 128 MiB of HBM per device.

v0:
```python
import functools

import jax
import jax.numpy as jnp
from jax import lax
from jax.experimental import pallas as pl
from jax.experimental.pallas import tpu as pltpu
from jax.sharding import PartitionSpec as P

SWEEPS = 4
WEIGHT = 0.8
AXES = ("gx", "gy", "gz")
MESH = pl.DeviceIdType.MESH
LANES = 128
PAD = 8
STEP = 8


def kernel(init_ref, rhs_hbm, shift_hbm, out_hbm, field, rhs, weight, z_out, z_in, load_sem, store_sem, send_sem, recv_sem):
    _, halves, planes, rows, _ = field.shape
    nx, ny = planes - 2, rows - 2 * PAD
    peers = {}
    for axis in AXES:
        me, size = lax.axis_index(axis), lax.axis_size(axis)
        peers[axis] = (lax.rem(me + 1, size), lax.rem(me + size - 1, size))

    loads = []
    for half in range(halves):
        lanes = pl.ds(half * LANES, LANES)
        loads.append((
            pltpu.make_async_copy(init_ref.at[:, :, lanes], field.at[0, half, pl.ds(1, nx), pl.ds(PAD, ny), :], load_sem.at[half, 0]),
            pltpu.make_async_copy(shift_hbm.at[:, :, lanes], weight.at[half], load_sem.at[half, 1]),
            pltpu.make_async_copy(rhs_hbm.at[:, :, lanes], rhs.at[half], load_sem.at[half, 2]),
        ))
    for which in range(3):
        for half in range(halves):
            loads[half][which].start()

    barrier = pltpu.get_barrier_semaphore()
    for axis in AXES:
        for peer in peers[axis]:
            pl.semaphore_signal(barrier, inc=1, device_id={axis: peer}, device_id_type=MESH)

    flat = field.reshape(2, halves, planes * rows, LANES)
    lane = lax.broadcasted_iota(jnp.int32, (ny, LANES), 1)
    nothing = jnp.zeros((ny, LANES), jnp.float32)

    def exchange(slot):
        copies = []
        for axis in AXES:
            for way in range(2):
                if axis == "gx":
                    src = field.at[slot, :, nx if way == 0 else 1, pl.ds(PAD, ny), :]
                    dst = field.at[slot, :, 0 if way == 0 else nx + 1, pl.ds(PAD, ny), :]
                elif axis == "gy":
                    src = field.at[slot, :, pl.ds(1, nx), pl.ds(PAD + ny - 1 if way == 0 else PAD, 1), :]
                    dst = field.at[slot, :, pl.ds(1, nx), pl.ds(PAD - 1 if way == 0 else PAD + ny, 1), :]
                else:
                    src, dst = z_out.at[slot, way], z_in.at[slot, way]
                which = 2 * AXES.index(axis) + way
                copies.append(pltpu.make_async_remote_copy(
                    src, dst, send_sem.at[slot, which], recv_sem.at[slot, which],
                    device_id={axis: peers[axis][way]}, device_id_type=MESH))
        return copies

    def pack(x, left, right, high, low):
        high = jnp.where(lane == x, pltpu.roll(right, lax.rem(x + 1, LANES), 1), high)
        low = jnp.where(lane == x, pltpu.roll(left, x, 1), low)
        return high, low

    for half in range(halves):
        loads[half][0].wait()

    def first_faces(trip, faces):
        for j in range(STEP):
            x = trip * STEP + j
            at = pl.ds(pl.multiple_of((x + 1) * rows + PAD, 8), ny)
            faces = pack(x, flat[0, 0, at, :], flat[0, halves - 1, at, :], *faces)
        return faces

    z_out[0, 0], z_out[0, 1] = lax.fori_loop(0, nx // STEP, first_faces, (nothing, nothing))
    pl.semaphore_wait(barrier, 2 * len(AXES))
    flying = exchange(0)
    for copy in flying:
        copy.start()

    for half in range(halves):
        loads[half][1].wait()

    @pl.loop(0, nx // STEP)
    def _(trip):
        at = pl.ds(pl.multiple_of(trip * STEP, STEP), STEP)
        for half in range(halves):
            weight[half, at] = WEIGHT / (6.0 + weight[half, at])

    for half in range(halves):
        loads[half][2].wait()

    stores = []
    for sweep in range(SWEEPS):
        old, new = sweep % 2, (sweep + 1) % 2
        for copy in flying:
            copy.wait()

        def planes_of(trip, faces):
            for j in range(STEP):
                x = trip * STEP + j
                base = pl.multiple_of((x + 1) * rows, 8)
                at = pl.ds(base + PAD, ny)
                here = [flat[old, half, at, :] for half in range(halves)]
                fore = [pltpu.roll(v, 1, 1) for v in here]
                back = [pltpu.roll(v, LANES - 1, 1) for v in here]
                low = pltpu.roll(z_in[old, 0], lax.rem(LANES - x, LANES), 1)
                high = pltpu.roll(z_in[old, 1], LANES - 1 - x, 1)
                fresh = []
                for half in range(halves):
                    before = jnp.where(lane == 0, low if half == 0 else fore[half - 1], fore[half])
                    after = jnp.where(lane == LANES - 1, high if half == halves - 1 else back[half + 1], back[half])
                    beside = before + after
                    beside = beside + (flat[old, half, pl.ds(base + PAD - 1, ny), :] + flat[old, half, pl.ds(base + PAD + 1, ny), :])
                    beside = beside + (flat[old, half, pl.ds(base + PAD - rows, ny), :] + flat[old, half, pl.ds(base + PAD + rows, ny), :])
                    value = (1.0 - WEIGHT) * here[half] + weight[half, x] * (rhs[half, x] + beside)
                    flat[new, half, at, :] = value
                    fresh.append(value)
                if sweep < SWEEPS - 1:
                    faces = pack(x, fresh[0], fresh[-1], *faces)
            return faces

        faces = lax.fori_loop(0, nx // STEP, planes_of, (nothing, nothing))
        if sweep < SWEEPS - 1:
            z_out[new, 0], z_out[new, 1] = faces
            flying = exchange(new)
            for copy in flying:
                copy.start()
    for half in range(halves):
        stores.append(pltpu.make_async_copy(
            field.at[SWEEPS % 2, half, pl.ds(1, nx), pl.ds(PAD, ny), :], out_hbm.at[:, :, pl.ds(half * LANES, LANES)], store_sem.at[half]))
    for copy in stores:
        copy.start()
    for copy in stores:
        copy.wait()


def relax(initial, right_side, shift_field):
    nx, ny, nz = initial.shape
    halves = nz // LANES
    block = (halves, nx, ny, LANES)
    return pl.pallas_call(
        kernel,
        out_shape=jax.ShapeDtypeStruct(initial.shape, jnp.float32),
        in_specs=[pl.BlockSpec(memory_space=pl.ANY)] * 3,
        out_specs=pl.BlockSpec(memory_space=pl.ANY),
        scratch_shapes=[
            pltpu.VMEM((2, halves, nx + 2, ny + 2 * PAD, LANES), jnp.float32),
            pltpu.VMEM(block, jnp.float32),
            pltpu.VMEM(block, jnp.float32),
            pltpu.VMEM((2, 2, ny, LANES), jnp.float32),
            pltpu.VMEM((2, 2, ny, LANES), jnp.float32),
            pltpu.SemaphoreType.DMA((halves, 3)),
            pltpu.SemaphoreType.DMA((halves,)),
            pltpu.SemaphoreType.DMA((2, 6)),
            pltpu.SemaphoreType.DMA((2, 6)),
        ],
        compiler_params=pltpu.CompilerParams(collective_id=0, has_side_effects=True),
    )(initial, right_side, shift_field)


def solution(mesh):
    return jax.shard_map(
        relax,
        mesh=mesh,
        in_specs=(P(*AXES), P(*AXES), P(*AXES)),
        out_specs=P(*AXES),
        check_vma=False,
    )
```

profile of v0, /device:TPU:1, one launch (start us, length us, event | category | flops | bytes accessed | tf_op | source)
XLA Modules:
  0.0 44.3 jit_solution(11898160197004554851)
XLA Ops:
  0.0 41.1 %shard_map.37 = f32[64,32,256]{2,1,0:T(8,128)} custom-call(f32[64,32,256]{2,1,0:T(8,128)} %init_ref.1, f32[64,32,256]{2,1,0:T(8,128)} %rhs_hbm.1, f32[64,32,256]{2,1,0:T(8,128)} %shift_hbm.1), custom_call_target="tpu_custom_call" | custom-call | tf_op jit(solution)/shard_map/pallas_call | solution.py:148
  41.1 3.2 %copy.5 = f32[64,32,256]{2,1,0:T(8,128)} copy(f32[64,32,256]{2,1,0:T(8,128)} %shard_map.37) | data formatting | bytes 4194304
where the time goes:
time: 44.8 us; the launch traced here: 44.3 us
  Pallas kernels  41.1 us (92%)
  local copies, waits for them, and re-layouts  3.16 us (7%)
    pallas_call x1, Pallas kernels, relax(): pl.pallas_call(kernel, out_shape=jax.ShapeDtypeStruct(initial.shape, jnp....  41.1 us
    unnamed x1, local copies, waits for them, and re-layouts  3.16 us

commit v1 on v0

v1 whole, which is shorter than its diff:
```python
import jax
import jax.numpy as jnp
from jax import lax
from jax.experimental import pallas as pl
from jax.experimental.pallas import tpu as pltpu
from jax.sharding import PartitionSpec as P

SWEEPS = 4
WEIGHT = 0.8
AXES = ("gx", "gy", "gz")
MESH = pl.DeviceIdType.MESH
LANES = 128
PAD = 8
STEP = 8


def kernel(
    init_hbm, rhs_hbm, shift_hbm, out_hbm, field_a, field_b, rhs, weight, weight_y, x_in, y_in, z_in, z_out,
    load_sem, store_sem, send_sem, recv_sem,
):
    halves, planes, rows, _ = field_a.shape
    nx, ny = planes - 2, rows - PAD
    last = halves - 1
    trips = nx // STEP
    field = (field_a, field_b)
    flat = tuple(f.reshape(halves, planes * rows, LANES) for f in field)
    peers = {}
    for axis in AXES:
        me, size = lax.axis_index(axis), lax.axis_size(axis)
        peers[axis] = (lax.rem(me + 1, size), lax.rem(me + size - 1, size))
    base = lax.rem(lax.axis_index("gx"), 2) * nx

    loads = []
    for source, place in ((init_hbm, field_b.at[:, pl.ds(1, nx), pl.ds(0, ny), :]), (shift_hbm, weight), (rhs_hbm, rhs)):
        which = len(loads)
        loads.append([
            pltpu.make_async_copy(source.at[:, :, pl.ds(half * LANES, LANES)], place.at[half], load_sem.at[half, which])
            for half in range(halves)
        ])
    for group in loads:
        for copy in group:
            copy.start()

    barrier = pltpu.get_barrier_semaphore()
    for axis in AXES:
        for peer in peers[axis]:
            pl.semaphore_signal(barrier, inc=1, device_id={axis: peer}, device_id_type=MESH)

    lane = lax.broadcasted_iota(jnp.int32, (ny, LANES), 1)
    behind = jnp.where(lane == LANES - 1, 0, lane + 1)
    nothing = jnp.zeros((ny, LANES), jnp.float32)

    def plane_at(x, shift=0):
        return pl.ds(pl.multiple_of((x + 1) * rows, 8) + shift, ny)

    for f in field:
        for half in range(halves):
            f[half, 0] = jnp.zeros((rows, LANES), jnp.float32)
            f[half, nx + 1] = jnp.zeros((rows, LANES), jnp.float32)

    @pl.loop(0, trips)
    def _(trip):
        for f in field:
            for half in range(halves):
                f[half, pl.ds(trip * STEP + 1, STEP), pl.ds(ny, PAD), :] = jnp.zeros((STEP, PAD, LANES), jnp.float32)

    def exchange(slot):
        copies = []
        for axis in AXES:
            for way in range(2):
                if axis == "gx":
                    src, dst = field[slot].at[:, nx if way == 0 else 1, pl.ds(0, ny), :], x_in.at[slot, way]
                elif axis == "gy":
                    src, dst = field[slot].at[:, pl.ds(1, nx), ny - 1 if way == 0 else 0, :], y_in.at[slot, way]
                else:
                    src, dst = z_out.at[slot, way], z_in.at[slot, way]
                which = 2 * AXES.index(axis) + way
                copies.append(pltpu.make_async_remote_copy(
                    src, dst, send_sem.at[slot, which], recv_sem.at[slot, which],
                    device_id={axis: peers[axis][way]}, device_id_type=MESH))
        return copies

    def pack(skew, faces, first, final):
        return jnp.where(behind == skew, final, faces[0]), jnp.where(lane == skew, first, faces[1])

    for copy in loads[0]:
        copy.wait()

    def rotate_field(trip, faces):
        for j in range(STEP):
            x = trip * STEP + j
            turned = [pltpu.roll(flat[1][half, plane_at(x), :], base + x, 1) for half in range(halves)]
            for half in range(halves):
                flat[0][half, plane_at(x), :] = turned[half]
            faces = pack(base + x, faces, turned[0], turned[last])
        return faces

    z_out[0, 0], z_out[0, 1] = lax.fori_loop(0, trips, rotate_field, (nothing, nothing))
    pl.semaphore_wait(barrier, 2 * len(AXES))
    flying = exchange(0)
    for copy in flying:
        copy.start()

    for copy in loads[1]:
        copy.wait()

    def rotate_weight(trip, faces):
        for j in range(STEP):
            x = trip * STEP + j
            turned = [WEIGHT / (6.0 + pltpu.roll(weight[half, x], base + x, 1)) for half in range(halves)]
            for half in range(halves):
                weight[half, x] = turned[half]
            faces = pack(base + x, faces, turned[0], turned[last])
        return faces

    weight_high, weight_low = lax.fori_loop(0, trips, rotate_weight, (nothing, nothing))
    z_weight = (weight_low, weight_high)
    for copy in loads[2]:
        copy.wait()

    @pl.loop(0, trips)
    def _(trip):
        for j in range(STEP):
            x = trip * STEP + j
            for half in range(halves):
                rhs[half, x] = pltpu.roll(rhs[half, x], base + x, 1)

    flat_weight = weight.reshape(halves, nx * ny, LANES)
    for side, row in ((0, 0), (1, ny - 1)):
        for half in range(halves):
            for x in range(0, nx, 8):
                weight_y[side, half, pl.ds(x, 8)] = flat_weight[half, pl.ds(x * ny + row, 8, stride=ny), :]

    for sweep in range(SWEEPS):
        old, new = sweep % 2, (sweep + 1) % 2

        @pl.loop(0, trips)
        def _(trip):
            for j in range(STEP):
                x = trip * STEP + j
                here = [flat[old][half, plane_at(x), :] for half in range(halves)]
                at_first, at_last = lane == base + x, behind == base + x
                for half in range(halves):
                    after = jnp.where(at_first, here[half + 1] if half < last else 0.0, here[half]) + flat[old][half, plane_at(x + 1), :]
                    before = jnp.where(at_last, here[half - 1] if half > 0 else 0.0, here[half]) + flat[old][half, plane_at(x - 1), :]
                    beside = flat[old][half, plane_at(x, -1), :] + flat[old][half, plane_at(x, 1), :] + rhs[half, x]
                    beside = beside + (pltpu.roll(after, LANES - 1, 1) + pltpu.roll(before, 1, 1))
                    flat[new][half, plane_at(x), :] = (1.0 - WEIGHT) * here[half] + weight[half, x] * beside

        for copy in flying:
            copy.wait()

        for way, x, turn in ((0, 0, 1), (1, nx - 1, LANES - 1)):
            for half in range(halves):
                flat[new][half, plane_at(x), :] += weight[half, x] * pltpu.roll(x_in[old, way, half], turn, 1)
        for way, row in ((0, 0), (1, ny - 1)):
            for half in range(halves):
                for x in range(0, nx, 8):
                    at = pl.ds((x + 1) * rows + row, 8, stride=rows)
                    flat[new][half, at, :] += weight_y[way, half, pl.ds(x, 8)] * y_in[old, way, half, pl.ds(x, 8)]
        add_low = z_weight[0] * pltpu.roll(z_in[old, 0], 1, 1)
        add_high = z_weight[1] * pltpu.roll(z_in[old, 1], LANES - 1, 1)

        def corrected(x):
            at_first, at_last = lane == base + x, behind == base + x
            values = [flat[new][half, plane_at(x), :] for half in range(halves)]
            values[0] = values[0] + jnp.where(at_first, add_low, 0.0)
            values[last] = values[last] + jnp.where(at_last, add_high, 0.0)
            return values

        if sweep < SWEEPS - 1:

            def finish(trip, faces):
                for j in range(STEP):
                    x = trip * STEP + j
                    values = corrected(x)
                    for half in range(halves):
                        flat[new][half, plane_at(x), :] = values[half]
                    faces = pack(base + x, faces, values[0], values[last])
                return faces

            z_out[new, 0], z_out[new, 1] = lax.fori_loop(0, trips, finish, (nothing, nothing))
            flying = exchange(new)
            for copy in flying:
                copy.start()

    def store(trip, half):
        some = pl.multiple_of(trip * STEP, STEP)
        return pltpu.make_async_copy(
            field[old].at[half, pl.ds(some + 1, STEP), pl.ds(0, ny), :],
            out_hbm.at[pl.ds(some, STEP), :, pl.ds(half * LANES, LANES)], store_sem.at[half, trip])

    @pl.loop(0, trips)
    def _(trip):
        for j in range(STEP):
            x = trip * STEP + j
            values = corrected(x)
            for half in range(halves):
                flat[old][half, plane_at(x), :] = pltpu.roll(values[half], lax.rem(LANES - base - x, LANES), 1)
        for half in range(halves):
            store(trip, half).start()

    @pl.loop(0, trips)
    def _(trip):
        for half in range(halves):
            store(trip, half).wait()


def relax(initial, right_side, shift_field):
    nx, ny, nz = initial.shape
    halves = nz // LANES
    plane = (ny, LANES)
    field = (halves, nx + 2, ny + PAD, LANES)
    f32 = jnp.float32
    return pl.pallas_call(
        kernel,
        out_shape=jax.ShapeDtypeStruct(initial.shape, f32),
        in_specs=[pl.BlockSpec(memory_space=pl.ANY)] * 3,
        out_specs=pl.BlockSpec(memory_space=pl.ANY),
        scratch_shapes=[
            pltpu.VMEM(field, f32),
            pltpu.VMEM(field, f32),
            pltpu.VMEM((halves, nx) + plane, f32),
            pltpu.VMEM((halves, nx) + plane, f32),
            pltpu.VMEM((2, halves, nx, LANES), f32),
            pltpu.VMEM((2, 2, halves) + plane, f32),
            pltpu.VMEM((2, 2, halves, nx, LANES), f32),
            pltpu.VMEM((2, 2) + plane, f32),
            pltpu.VMEM((2, 2) + plane, f32),
            pltpu.SemaphoreType.DMA((halves, 3)),
            pltpu.SemaphoreType.DMA((halves, nx // STEP)),
            pltpu.SemaphoreType.DMA((2, 6)),
            pltpu.SemaphoreType.DMA((2, 6)),
        ],
        compiler_params=pltpu.CompilerParams(collective_id=0, has_side_effects=True),
    )(initial, right_side, shift_field)


def solution(mesh):
    return jax.shard_map(
        relax,
        mesh=mesh,
        in_specs=(P(*AXES), P(*AXES), P(*AXES)),
        out_specs=P(*AXES),
        check_vma=False,
    )
```

time: 44.8 us -> 29 us (0.65)
  the two profiles are of different devices: /device:TPU:1 before, /device:TPU:2 now
where the time goes in v1:
time: 29 us; the launch traced here: 28.9 us
  Pallas kernels  25.8 us (89%)
  local copies, waits for them, and re-layouts  3.16 us (11%)
    pallas_call x1, Pallas kernels, relax(): pl.pallas_call(kernel, out_shape=jax.ShapeDtypeStruct(initial.shape, f32)...  25.8 us
    unnamed x1, local copies, waits for them, and re-layouts  3.16 us

profile of v1, /device:TPU:2, one launch (start us, length us, event | category | flops | bytes accessed | tf_op | source)
XLA Modules:
  0.0 28.9 jit_solution(13247314562844704909)
XLA Ops:
  0.0 25.8 %shard_map.37 = f32[64,32,256]{2,1,0:T(8,128)} custom-call(f32[64,32,256]{2,1,0:T(8,128)} %init_hbm.1, f32[64,32,256]{2,1,0:T(8,128)} %rhs_hbm.1, f32[64,32,256]{2,1,0:T(8,128)} %shift_hbm.1), custom_call_target="tpu_custom_call" | custom-call | tf_op jit(solution)/shard_map/pallas_call | solution.py:215
  25.8 3.2 %copy.5 = f32[64,32,256]{2,1,0:T(8,128)} copy(f32[64,32,256]{2,1,0:T(8,128)} %shard_map.37) | data formatting | bytes 4194304

commit v2 on v1

--- a/solution.py
+++ b/solution.py
@@ -15,8 +15,8 @@
 
 
 def kernel(
-    init_hbm, rhs_hbm, shift_hbm, out_hbm, field_a, field_b, rhs, weight, weight_y, x_in, y_in, z_in, z_out,
-    load_sem, store_sem, send_sem, recv_sem,
+    init_hbm, rhs_hbm, shift_hbm, out, field_a, field_b, rhs, weight, weight_y, x_in, y_in, z_in, z_out,
+    load_sem, send_sem, recv_sem,
 ):
     halves, planes, rows, _ = field_a.shape
     nx, ny = planes - 2, rows - PAD
@@ -184,26 +184,13 @@
             for copy in flying:
                 copy.start()
 
-    def store(trip, half):
-        some = pl.multiple_of(trip * STEP, STEP)
-        return pltpu.make_async_copy(
-            field[old].at[half, pl.ds(some + 1, STEP), pl.ds(0, ny), :],
-            out_hbm.at[pl.ds(some, STEP), :, pl.ds(half * LANES, LANES)], store_sem.at[half, trip])
-
     @pl.loop(0, trips)
     def _(trip):
         for j in range(STEP):
             x = trip * STEP + j
             values = corrected(x)
             for half in range(halves):
-                flat[old][half, plane_at(x), :] = pltpu.roll(values[half], lax.rem(LANES - base - x, LANES), 1)
-        for half in range(halves):
-            store(trip, half).start()
-
-    @pl.loop(0, trips)
-    def _(trip):
-        for half in range(halves):
-            store(trip, half).wait()
+                out[x, :, half * LANES:(half + 1) * LANES] = pltpu.roll(values[half], lax.rem(LANES - base - x, LANES), 1)
 
 
 def relax(initial, right_side, shift_field):
@@ -215,8 +202,8 @@
     return pl.pallas_call(
         kernel,
         out_shape=jax.ShapeDtypeStruct(initial.shape, f32),
-        in_specs=[pl.BlockSpec(memory_space=pl.ANY)] * 3,
-        out_specs=pl.BlockSpec(memory_space=pl.ANY),
+        in_specs=[pl.BlockSpec(memory_space=pltpu.HBM)] * 3,
+        out_specs=pl.BlockSpec(memory_space=pltpu.VMEM),
         scratch_shapes=[
             pltpu.VMEM(field, f32),
             pltpu.VMEM(field, f32),
@@ -228,12 +215,11 @@
             pltpu.VMEM((2, 2) + plane, f32),
             pltpu.VMEM((2, 2) + plane, f32),
             pltpu.SemaphoreType.DMA((halves, 3)),
-            pltpu.SemaphoreType.DMA((halves, nx // STEP)),
             pltpu.SemaphoreType.DMA((2, 6)),
             pltpu.SemaphoreType.DMA((2, 6)),
         ],
-        compiler_params=pltpu.CompilerParams(collective_id=0, has_side_effects=True),
-    )(initial, right_side, shift_field)
+        compiler_params=pltpu.CompilerParams(collective_id=0, has_side_effects=True, vmem_limit_bytes=24 * 2**20),
+    )(*(pltpu.with_memory_space_constraint(a, pltpu.HBM) for a in (initial, right_side, shift_field)))
 
 
 def solution(mesh):

time: 29 us -> 26.3 us (0.907)
  local copies, waits for them, and re-layouts: 3.16 us -> 1.32 us
  Pallas kernels: 25.8 us -> 24.9 us
    unnamed x1, local copies, waits for them, and re-layouts: 3.16 us -> 1.32 us
    pallas_call x1, Pallas kernels: 25.8 us -> 24.9 us  [relax(): pl.pallas_call(kernel, out_shape=jax.ShapeDtypeStruct(initial.shape, f32)...]
where the time goes in v2:
time: 26.3 us; the launch traced here: 26.2 us
  Pallas kernels  24.9 us (95%)
  local copies, waits for them, and re-layouts  1.32 us (5%)
    pallas_call x1, Pallas kernels, relax(): pl.pallas_call(kernel, out_shape=jax.ShapeDtypeStruct(initial.shape, f32)...  24.9 us
    unnamed x1, local copies, waits for them, and re-layouts  1.32 us

profile of v2, /device:TPU:2, one launch (start us, length us, event | category | flops | bytes accessed | tf_op | source)
XLA Modules:
  0.0 26.2 jit_solution(9147000045439798396)
XLA Ops:
  0.0 24.9 %shard_map.37 = f32[64,32,256]{2,1,0:T(8,128)S(1)} custom-call(f32[64,32,256]{2,1,0:T(8,128)} %init_hbm.1, f32[64,32,256]{2,1,0:T(8,128)} %rhs_hbm.1, f32[64,32,256]{2,1,0:T(8,128)} %shift_hbm.1), custom_call_target="tpu_custom_call" | custom-call | tf_op jit(solution)/shard_map/pallas_call | solution.py:202
  24.9 1.3 %copy.5 = f32[64,32,256]{2,1,0:T(8,128)} copy(f32[64,32,256]{2,1,0:T(8,128)S(1)} %shard_map.37) | data formatting | bytes 4194304

commit v3 on v2

v3 whole, which is shorter than its diff:
```python
import jax
import jax.numpy as jnp
from jax import lax
from jax.experimental import pallas as pl
from jax.experimental.pallas import tpu as pltpu
from jax.sharding import PartitionSpec as P

SWEEPS = 4
WEIGHT = 0.8
KEEP = 1.0 - WEIGHT
AXES = ("gx", "gy", "gz")
MESH = pl.DeviceIdType.MESH
LANES = 128
PAD = 8
STEP = 16


def kernel(
    init_hbm, rhs_hbm, shift_hbm, out, field_a, field_b, field_c, rhs, weight, weight_y, rhs_y, z_coef, z_out, x_in, y_in, z_in,
    x_near, x_far, y_near, y_far, z_near, z_far, xy_in, xz_in, yz_in, x_coef, y_coef, z_coef_in, x_add, y_add, z_add,
    load_sem, send_sem, recv_sem, deep_send, deep_recv, coef_send, coef_recv,
):
    halves, planes, rows, _ = field_a.shape
    nx, ny = planes - 2, rows - PAD
    last = halves - 1
    trips = nx // STEP
    field = (field_a, field_b, field_c)
    flat = tuple(f.reshape(halves, planes * rows, LANES) for f in field)
    peers = {}
    for axis in AXES:
        me, size = lax.axis_index(axis), lax.axis_size(axis)
        peers[axis] = (lax.rem(me + 1, size), lax.rem(me + size - 1, size))
    base = lax.rem(lax.axis_index("gx"), 2) * nx
    sides = ((0, 1), (1, LANES - 1))

    loads = []
    for source, place in ((init_hbm, field_b.at[:, pl.ds(1, nx), pl.ds(0, ny), :]), (shift_hbm, weight), (rhs_hbm, rhs)):
        which = len(loads)
        loads.append([
            pltpu.make_async_copy(source.at[:, :, pl.ds(half * LANES, LANES)], place.at[half], load_sem.at[half, which])
            for half in range(halves)
        ])
    for group in loads:
        for copy in group:
            copy.start()

    barrier = pltpu.get_barrier_semaphore()
    for axis in AXES:
        for peer in peers[axis]:
            pl.semaphore_signal(barrier, inc=1, device_id={axis: peer}, device_id_type=MESH)

    lane = lax.broadcasted_iota(jnp.int32, (ny, LANES), 1)
    behind = jnp.where(lane == LANES - 1, 0, lane + 1)
    behind_two = jnp.where(behind == LANES - 1, 0, behind + 1)
    ahead = jnp.where(lane == 0, LANES - 1, lane - 1)
    nothing = jnp.zeros((ny, LANES), jnp.float32)

    def plane_at(x, shift=0):
        return pl.ds(pl.multiple_of((x + 1) * rows, 8) + shift, ny)

    def row_at(x, row):
        return pl.ds((x + 1) * rows + row, 8, stride=rows)

    for f in field[:2]:
        for half in range(halves):
            f[half, 0] = jnp.zeros((rows, LANES), jnp.float32)
            f[half, nx + 1] = jnp.zeros((rows, LANES), jnp.float32)

    @pl.loop(0, trips)
    def _(trip):
        for f in field[:2]:
            for half in range(halves):
                f[half, pl.ds(trip * STEP + 1, STEP), pl.ds(ny, PAD), :] = jnp.zeros((STEP, PAD, LANES), jnp.float32)

    edge = jnp.zeros((PAD, LANES), jnp.float32)
    for way in range(2):
        for half in range(halves):
            for ref, size in ((x_add.at[way, half], ny), (y_add.at[way, half], nx)):
                ref[pl.ds(0, PAD)] = edge
                ref[pl.ds(PAD + size, PAD)] = edge
        z_add[way, pl.ds(0, PAD)] = edge
        z_add[way, pl.ds(PAD + ny, PAD)] = edge

    def send(src, dst, sems, which, target):
        return pltpu.make_async_remote_copy(
            src, dst, sems[0].at[which], sems[1].at[which], device_id=target, device_id_type=MESH)

    def exchange(slot):
        copies = []
        for axis in AXES:
            for way in range(2):
                if axis == "gx":
                    src, dst = field[slot].at[:, nx if way == 0 else 1, pl.ds(0, ny), :], x_in.at[slot, way]
                elif axis == "gy":
                    src, dst = field[slot].at[:, pl.ds(1, nx), ny - 1 if way == 0 else 0, :], y_in.at[slot, way]
                else:
                    src, dst = z_out.at[slot, 0, way], z_in.at[slot, way]
                which = 6 * slot + 2 * AXES.index(axis) + way
                copies.append(send(src, dst, (send_sem, recv_sem), which, {axis: peers[axis][way]}))
        return copies

    def deep_exchange(slot):
        near, far, around = [], [], []
        f = field[slot]

        def add(group, src, dst, target):
            which = len(near) + len(far) + len(around)
            group.append(send(src, dst, (deep_send, deep_recv), which, target))

        for way in range(2):
            up = way == 0
            target = {axis: {axis: peers[axis][way]} for axis in AXES}
            add(near, f.at[:, nx if up else 1, pl.ds(0, ny), :], x_near.at[way, :, pl.ds(PAD, ny), :], target["gx"])
            add(near, f.at[:, pl.ds(1, nx), ny - 1 if up else 0, :], y_near.at[way, :, pl.ds(PAD, nx), :], target["gy"])
            add(near, z_out.at[slot, 0, way], z_near.at[way, pl.ds(PAD, ny), :], target["gz"])
            add(far, f.at[:, nx - 1 if up else 2, pl.ds(0, ny), :], x_far.at[way], target["gx"])
            add(far, f.at[:, pl.ds(1, nx), ny - 2 if up else 1, :], y_far.at[way], target["gy"])
            add(far, z_out.at[slot, 1, way], z_far.at[way], target["gz"])
            for other in range(2):
                row = pl.ds(ny - 1 if other == 0 else 0, 1)
                add(around, f.at[:, nx if up else 1, row, :], xy_in.at[way, other, :, pl.ds(0, 1), :],
                    {"gx": peers["gx"][way], "gy": peers["gy"][other]})
                add(around, z_out.at[slot, 0, other], xz_in.at[way, other], {"gx": peers["gx"][way], "gz": peers["gz"][other]})
                row = pl.ds(ny - 1 if up else 0, 1)
                add(around, z_out.at[slot, 0, other, row, :], yz_in.at[way, other, pl.ds(0, 1), :],
                    {"gy": peers["gy"][way], "gz": peers["gz"][other]})
        return around + near + far

    def coefficients(kind):
        copies = []
        whole, lines = ((weight, weight_y), (rhs, rhs_y))[kind]
        for way in range(2):
            for axis, src, dst in (
                ("gx", whole.at[:, nx - 1 if way == 0 else 0], x_coef.at[kind, way]),
                ("gy", lines.at[0, 1 - way], y_coef.at[kind, way]),
                ("gz", z_coef.at[kind, way], z_coef_in.at[kind, way]),
            ):
                which = 6 * kind + 2 * AXES.index(axis) + way
                copies.append(send(src, dst, (coef_send, coef_recv), which, {axis: peers[axis][way]}))
        return copies

    def pack(skew, faces, first, final):
        return jnp.where(behind == skew, final, faces[0]), jnp.where(lane == skew, first, faces[1])

    for copy in loads[0]:
        copy.wait()

    def rotate_field(trip, faces):
        for j in range(STEP):
            x = trip * STEP + j
            turned = [pltpu.roll(flat[1][half, plane_at(x), :], base + x, 1) for half in range(halves)]
            for half in range(halves):
                flat[0][half, plane_at(x), :] = turned[half]
            faces = pack(base + x, faces, turned[0], turned[last])
        return faces

    z_out[0, 0, 0], z_out[0, 0, 1] = lax.fori_loop(0, trips, rotate_field, (nothing, nothing))
    pl.semaphore_wait(barrier, 2 * len(AXES))
    flying = exchange(0)
    for copy in flying:
        copy.start()

    def second(skew):
        return ahead == skew, behind_two == skew

    for copy in loads[1]:
        copy.wait()

    def rotate_weight(trip, faces):
        for j in range(STEP):
            x = trip * STEP + j
            turned = [WEIGHT / (6.0 + pltpu.roll(weight[half, x], base + x, 1)) for half in range(halves)]
            for half in range(halves):
                weight[half, x] = turned[half]
            next_low, next_high = second(base + x)
            faces = pack(base + x, faces[:2], turned[0], turned[last]) + (
                jnp.where(next_high, turned[last], faces[2]), jnp.where(next_low, turned[0], faces[3]))
        return faces

    z_coef[0, 0], z_coef[0, 1], inner_high, inner_low = lax.fori_loop(0, trips, rotate_weight, (nothing,) * 4)
    z_coef[2, 0], z_coef[2, 1] = inner_high, inner_low

    def lines_of(values, lines, inner):
        by_row = values.reshape(halves, nx * ny, LANES)
        for side in range(2):
            row = ny - 1 - inner if side else inner
            for half in range(halves):
                for x in range(0, nx, 8):
                    lines[inner, side, half, pl.ds(x, 8)] = by_row[half, pl.ds(x * ny + row, 8, stride=ny), :]

    lines_of(weight, weight_y, 0)
    for copy in loads[2]:
        copy.wait()

    def rotate_rhs(trip, faces):
        for j in range(STEP):
            x = trip * STEP + j
            turned = [pltpu.roll(rhs[half, x], base + x, 1) for half in range(halves)]
            for half in range(halves):
                rhs[half, x] = turned[half]
            faces = pack(base + x, faces, turned[0], turned[last])
        return faces

    z_coef[1, 0], z_coef[1, 1] = lax.fori_loop(0, trips, rotate_rhs, (nothing, nothing))

    def sweep_inside(old, new):
        @pl.loop(0, trips)
        def _(trip):
            for j in range(STEP):
                x = trip * STEP + j
                here = [flat[old][half, plane_at(x), :] for half in range(halves)]
                at_first, at_last = lane == base + x, behind == base + x
                for half in range(halves):
                    after = jnp.where(at_first, here[half + 1] if half < last else 0.0, here[half]) + flat[old][half, plane_at(x + 1), :]
                    before = jnp.where(at_last, here[half - 1] if half > 0 else 0.0, here[half]) + flat[old][half, plane_at(x - 1), :]
                    beside = flat[old][half, plane_at(x, -1), :] + flat[old][half, plane_at(x, 1), :] + rhs[half, x]
                    beside = beside + (pltpu.roll(after, LANES - 1, 1) + pltpu.roll(before, 1, 1))
                    flat[new][half, plane_at(x), :] = KEEP * here[half] + weight[half, x] * beside

    for sweep in range(SWEEPS - 2):
        old, new = sweep % 2, (sweep + 1) % 2
        if sweep == 1:
            lines_of(weight, weight_y, 1)
            lines_of(rhs, rhs_y, 0)
            sent = coefficients(0) + coefficients(1)
            for copy in sent:
                copy.start()
        sweep_inside(old, new)
        for copy in flying:
            copy.wait()

        for way, turn in sides:
            x = (0, nx - 1)[way]
            for half in range(halves):
                flat[new][half, plane_at(x), :] += weight[half, x] * pltpu.roll(x_in[old, way, half], turn, 1)
        for way, _ in sides:
            for half in range(halves):
                for x in range(0, nx, 8):
                    at = row_at(x, (0, ny - 1)[way])
                    flat[new][half, at, :] += weight_y[0, way, half, pl.ds(x, 8)] * y_in[old, way, half, pl.ds(x, 8)]
        add_low = z_coef[0, 1] * pltpu.roll(z_in[old, 0], 1, 1)
        add_high = z_coef[0, 0] * pltpu.roll(z_in[old, 1], LANES - 1, 1)
        deep = sweep == SWEEPS - 3

        def finish(trip, faces):
            for j in range(STEP):
                x = trip * STEP + j
                at_first, at_last = lane == base + x, behind == base + x
                values = [flat[new][half, plane_at(x), :] for half in range(halves)]
                values[0] = values[0] + jnp.where(at_first, add_low, 0.0)
                values[last] = values[last] + jnp.where(at_last, add_high, 0.0)
                for half in range(halves):
                    flat[new][half, plane_at(x), :] = values[half]
                packed = pack(base + x, faces[:2], values[0], values[last])
                if deep:
                    next_low, next_high = second(base + x)
                    packed += (jnp.where(next_high, values[last], faces[2]), jnp.where(next_low, values[0], faces[3]))
                faces = packed
            return faces

        faces = lax.fori_loop(0, trips, finish, (nothing,) * (4 if deep else 2))
        z_out[new, 0, 0], z_out[new, 0, 1] = faces[:2]
        if deep:
            z_out[new, 1, 0], z_out[new, 1, 1] = faces[2:]
        flying = deep_exchange(new) if deep else exchange(new)
        for copy in flying:
            copy.start()

    sweep_inside(0, 1)
    sweep_inside(1, 2)
    for copy in flying + sent:
        copy.wait()

    outside = (lax.rem(base + LANES - 1, LANES), lax.rem(base + nx, LANES))

    def along_plane(buf, skew, below, above):
        sums = []
        here = [buf[half, pl.ds(PAD, ny)] for half in range(halves)]
        for half in range(halves):
            after = jnp.where(lane == skew, here[half + 1] if half < last else above, here[half])
            before = jnp.where(behind == skew, here[half - 1] if half > 0 else below, here[half])
            sums.append(
                (buf[half, pl.ds(PAD - 1, ny)] + buf[half, pl.ds(PAD + 1, ny)])
                + (pltpu.roll(after, LANES - 1, 1) + pltpu.roll(before, 1, 1)))
        return sums

    tall = lax.broadcasted_iota(jnp.int32, (nx, LANES), 1)
    plane_skew = lax.broadcasted_iota(jnp.int32, (nx, LANES), 0) + base
    tall_first = tall == plane_skew
    tall_last = jnp.where(tall == LANES - 1, 0, tall + 1) == plane_skew

    def along_lines(buf, below, above):
        sums = []
        here = [buf[half, pl.ds(PAD, nx)] for half in range(halves)]
        for half in range(halves):
            after = jnp.where(tall_first, here[half + 1] if half < last else above, here[half]) + buf[half, pl.ds(PAD + 1, nx)]
            before = jnp.where(tall_last, here[half - 1] if half > 0 else below, here[half]) + buf[half, pl.ds(PAD - 1, nx)]
            sums.append(pltpu.roll(after, LANES - 1, 1) + pltpu.roll(before, 1, 1))
        return sums

    def along_columns(buf, here):
        return (buf[pl.ds(PAD - 1, ny)] + buf[pl.ds(PAD + 1, ny)]) + (pltpu.roll(here, LANES - 1, 1) + pltpu.roll(here, 1, 1))

    for way in range(2):
        for other in range(2):
            for half in range(halves):
                line = xy_in[way, other, half, pl.ds(0, 1)]
                x_near[way, half, pl.ds((PAD - 1, PAD + ny)[other], 1)] = line
                y_near[other, half, pl.ds((PAD - 1, PAD + nx)[way], 1)] = line
            z_near[other, pl.ds((PAD - 1, PAD + ny)[way], 1)] = yz_in[way, other, pl.ds(0, 1)]

    z_total, z_inner = [], []
    for way, turn in sides:
        back = LANES - turn
        edge_x, edge_y = (0, nx - 1)[way], (0, ny - 1)[way]
        inner_x, inner_y = (1, nx - 2)[way], (1, ny - 2)[way]

        ring = along_plane(x_near.at[way], outside[way], xz_in[way, 0], xz_in[way, 1])
        for half in range(halves):
            near = x_near[way, half, pl.ds(PAD, ny)]
            beyond = ring[half] + x_coef[1, way, half]
            beyond = beyond + (pltpu.roll(x_far[way, half], turn, 1) + pltpu.roll(flat[0][half, plane_at(edge_x), :], back, 1))
            ring[half] = pltpu.roll(KEEP * near + x_coef[0, way, half] * beyond, turn, 1)
            x_add[way, half, pl.ds(PAD, ny)] = weight[half, edge_x] * pltpu.roll(near, turn, 1)
        spread = along_plane(x_add.at[way], base + edge_x, 0.0, 0.0)
        for half in range(halves):
            late = x_add[way, half, pl.ds(PAD, ny)]
            flat[2][half, plane_at(edge_x), :] += weight[half, edge_x] * (ring[half] + spread[half]) + KEEP * late
            flat[2][half, plane_at(inner_x), :] += weight[half, inner_x] * pltpu.roll(late, turn, 1)

        ring = along_lines(y_near.at[way], yz_in[way, 0, pl.ds(0, 1)], yz_in[way, 1, pl.ds(0, 1)])
        for half in range(halves):
            near = y_near[way, half, pl.ds(PAD, nx)]
            own = jnp.concatenate([flat[0][half, row_at(x, edge_y), :] for x in range(0, nx, 8)], axis=0)
            beyond = ring[half] + y_coef[1, way, half] + (y_far[way, half] + own)
            ring[half] = KEEP * near + y_coef[0, way, half] * beyond
            y_add[way, half, pl.ds(PAD, nx)] = weight_y[0, way, half] * near
        spread = along_lines(y_add.at[way], 0.0, 0.0)
        for half in range(halves):
            late = y_add[way, half, pl.ds(PAD, nx)]
            outer = weight_y[0, way, half] * (ring[half] + spread[half]) + KEEP * late
            inner = weight_y[1, way, half] * late
            for x in range(0, nx, 8):
                flat[2][half, row_at(x, edge_y), :] += outer[x:x + 8]
                flat[2][half, row_at(x, inner_y), :] += inner[x:x + 8]

        place = (behind, lane)[way]
        near = z_near[way, pl.ds(PAD, ny)]
        full = jnp.where(place == outside[0], xz_in[0, way], jnp.where(place == outside[1], xz_in[1, way], near))
        beyond = along_columns(z_near.at[way], full) + z_coef_in[1, way]
        beyond = beyond + (pltpu.roll(z_far[way], turn, 1) + pltpu.roll(z_out[0, 0, 1 - way], back, 1))
        ring = pltpu.roll(KEEP * near + z_coef_in[0, way] * beyond, turn, 1)
        late = z_coef[0, 1 - way] * pltpu.roll(near, turn, 1)
        z_add[way, pl.ds(PAD, ny)] = late
        z_total.append(z_coef[0, 1 - way] * (ring + along_columns(z_add.at[way], late)) + KEEP * late)
        z_inner.append(z_coef[2, 1 - way] * pltpu.roll(late, turn, 1))

    @pl.loop(0, trips)
    def _(trip):
        for j in range(STEP):
            x = trip * STEP + j
            next_low, next_high = second(base + x)
            turn = LANES - base - x if j else lax.rem(LANES - base - x, LANES)
            values = [flat[2][half, plane_at(x), :] for half in range(halves)]
            values[0] = values[0] + jnp.where(lane == base + x, z_total[0], jnp.where(next_low, z_inner[0], 0.0))
            values[last] = values[last] + jnp.where(behind == base + x, z_total[1], jnp.where(next_high, z_inner[1], 0.0))
            for half in range(halves):
                out[x, :, half * LANES:(half + 1) * LANES] = pltpu.roll(values[half], turn, 1)


def relax(initial, right_side, shift_field):
    nx, ny, nz = initial.shape
    halves = nz // LANES
    plane, padded = (ny, LANES), (ny + 2 * PAD, LANES)
    layer = (nx, LANES)
    field = (halves, nx + 2, ny + PAD, LANES)
    shapes = [
        field, field, field, (halves, nx) + plane, (halves, nx) + plane, (2, 2, halves) + layer, (1, 2, halves) + layer,
        (3, 2) + plane, (2, 2, 2) + plane,
        (2, 2, halves) + plane, (2, 2, halves) + layer, (2, 2) + plane,
        (2, halves) + padded, (2, halves) + plane, (2, halves, nx + 2 * PAD, LANES), (2, halves) + layer, (2,) + padded, (2,) + plane,
        (2, 2, halves, PAD, LANES), (2, 2) + plane, (2, 2, PAD, LANES),
        (2, 2, halves) + plane, (2, 2, halves) + layer, (2, 2) + plane,
        (2, halves) + padded, (2, halves, nx + 2 * PAD, LANES), (2,) + padded,
    ]
    dma = pltpu.SemaphoreType.DMA
    return pl.pallas_call(
        kernel,
        out_shape=jax.ShapeDtypeStruct(initial.shape, jnp.float32),
        in_specs=[pl.BlockSpec(memory_space=pltpu.HBM)] * 3,
        out_specs=pl.BlockSpec(memory_space=pltpu.VMEM),
        scratch_shapes=[pltpu.VMEM(shape, jnp.float32) for shape in shapes]
        + [dma((halves, 3)), dma((12,)), dma((12,)), dma((24,)), dma((24,)), dma((12,)), dma((12,))],
        compiler_params=pltpu.CompilerParams(collective_id=0, has_side_effects=True, vmem_limit_bytes=32 * 2**20),
    )(*(pltpu.with_memory_space_constraint(a, pltpu.HBM) for a in (initial, right_side, shift_field)))


def solution(mesh):
    return jax.shard_map(
        relax,
        mesh=mesh,
        in_specs=(P(*AXES), P(*AXES), P(*AXES)),
        out_specs=P(*AXES),
        check_vma=False,
    )
```

time: 26.3 us -> 25.1 us (0.954)
  the two profiles are of different devices: /device:TPU:2 before, /device:TPU:1 now
where the time goes in v3:
time: 25.1 us
  Pallas kernels  23.7 us (94%)
  local copies, waits for them, and re-layouts  1.32 us (5%)
    pallas_call x1, Pallas kernels, relax(): pl.pallas_call(kernel, out_shape=jax.ShapeDtypeStruct(initial.shape, jnp....  23.7 us
    unnamed x1, local copies, waits for them, and re-layouts  1.32 us

profile of v3, /device:TPU:1, one launch (start us, length us, event | category | flops | bytes accessed | tf_op | source)
XLA Modules:
  0.0 25.1 jit_solution(5874650808168048299)
XLA Ops:
  0.0 23.7 %shard_map.37 = f32[64,32,256]{2,1,0:T(8,128)S(1)} custom-call(f32[64,32,256]{2,1,0:T(8,128)} %init_hbm.1, f32[64,32,256]{2,1,0:T(8,128)} %rhs_hbm.1, f32[64,32,256]{2,1,0:T(8,128)} %shift_hbm.1), custom_call_target="tpu_custom_call" | custom-call | tf_op jit(solution)/shard_map/pallas_call | solution.py:387
  23.7 1.3 %copy.5 = f32[64,32,256]{2,1,0:T(8,128)} copy(f32[64,32,256]{2,1,0:T(8,128)S(1)} %shard_map.37) | data formatting | bytes 4194304

commit v4 on v3

v4 whole, which is shorter than its diff:
```python
import jax
import jax.numpy as jnp
from jax import lax
from jax.experimental import pallas as pl
from jax.experimental.pallas import tpu as pltpu
from jax.sharding import PartitionSpec as P

SWEEPS = 4
WEIGHT = 0.8
KEEP = 1.0 - WEIGHT
AXES = ("gx", "gy", "gz")
MESH = pl.DeviceIdType.MESH
LANES = 128
PAD = 8
STEP = 16
INNER, OUTER = 20, 32


def kernel(
    init_hbm, rhs_hbm, shift_hbm, out, field_a, field_b, field_c, rhs, weight, weight_y, rhs_y, z_coef, z_out, x_in, y_in, z_in,
    x_near, x_far, y_near, y_far, z_near, z_far, xy_in, xz_in, yz_in, x_coef, y_coef, z_coef_in, x_add, y_add, z_add,
    load_sem, send_sem, recv_sem,
):
    halves, planes, rows, _ = field_a.shape
    nx, ny = planes - 2, rows - PAD
    last = halves - 1
    trips = nx // STEP
    field = (field_a, field_b, field_c)
    flat = tuple(f.reshape(halves, planes * rows, LANES) for f in field)
    peers = {}
    for axis in AXES:
        me, size = lax.axis_index(axis), lax.axis_size(axis)
        peers[axis] = (lax.rem(me + 1, size), lax.rem(me + size - 1, size))
    base = lax.rem(lax.axis_index("gx"), 2) * nx
    sides = ((0, 1), (1, LANES - 1))

    all_planes = rhs.reshape(halves * nx, ny, LANES)
    face, layer_planes = halves, halves * nx // ny

    def wait_planes(sem, count):
        some = all_planes.at[pl.ds(0, count)]
        pltpu.make_async_copy(some, some, sem).wait()

    def wait_lines(sem, count):
        some = all_planes.at[0, pl.ds(0, count)]
        pltpu.make_async_copy(some, some, sem).wait()

    def load_part(trip):
        some = trip * STEP
        return [
            pltpu.make_async_copy(
                init_hbm.at[pl.ds(some, STEP), :, pl.ds(half * LANES, LANES)],
                field_b.at[half, pl.ds(some + 1, STEP), pl.ds(0, ny), :], load_sem.at[trip])
            for half in range(halves)
        ]

    loads = [
        [
            pltpu.make_async_copy(source.at[:, :, pl.ds(half * LANES, LANES)], place.at[half], load_sem.at[trips + which])
            for half in range(halves)
        ]
        for which, (source, place) in enumerate(((shift_hbm, weight), (rhs_hbm, rhs)))
    ]
    for trip in range(trips):
        for copy in load_part(trip):
            copy.start()
    for group in loads:
        for copy in group:
            copy.start()
    barrier = pltpu.get_barrier_semaphore()
    for axis in AXES:
        for peer in peers[axis]:
            pl.semaphore_signal(barrier, inc=1, device_id={axis: peer}, device_id_type=MESH)

    lane = lax.broadcasted_iota(jnp.int32, (ny, LANES), 1)
    behind = jnp.where(lane == LANES - 1, 0, lane + 1)
    behind_two = jnp.where(behind == LANES - 1, 0, behind + 1)
    ahead = jnp.where(lane == 0, LANES - 1, lane - 1)
    nothing = jnp.zeros((ny, LANES), jnp.float32)
    tall = lax.broadcasted_iota(jnp.int32, (nx, LANES), 1)
    plane_skew = lax.broadcasted_iota(jnp.int32, (nx, LANES), 0) + base
    tall_first = tall == plane_skew
    tall_last = jnp.where(tall == LANES - 1, 0, tall + 1) == plane_skew
    tall_second = jnp.where(tall == 0, LANES - 1, tall - 1) == plane_skew
    tall_last_but_one = jnp.where(tall >= LANES - 2, tall - (LANES - 2), tall + 2) == plane_skew

    def plane_at(x, shift=0):
        return pl.ds(pl.multiple_of((x + 1) * rows, 8) + shift, ny)

    def row_at(x, row):
        return pl.ds((x + 1) * rows + row, 8, stride=rows)

    for f in field[:2]:
        for half in range(halves):
            f[half, 0] = jnp.zeros((rows, LANES), jnp.float32)
            f[half, nx + 1] = jnp.zeros((rows, LANES), jnp.float32)

    @pl.loop(0, trips)
    def _(trip):
        for f in field[:2]:
            for half in range(halves):
                f[half, pl.ds(trip * STEP + 1, STEP), pl.ds(ny, PAD), :] = jnp.zeros((STEP, PAD, LANES), jnp.float32)

    edge = jnp.zeros((PAD, LANES), jnp.float32)
    for way in range(2):
        for half in range(halves):
            for ref, size in ((x_add.at[way, half], ny), (y_add.at[way, half], nx)):
                ref[pl.ds(0, PAD)] = edge
                ref[pl.ds(PAD + size, PAD)] = edge
        z_add[way, pl.ds(0, PAD)] = edge
        z_add[way, pl.ds(PAD + ny, PAD)] = edge

    def send(src, dst, sent, received, target):
        pltpu.make_async_remote_copy(
            src, dst, send_sem.at[sent], recv_sem.at[received], device_id=target, device_id_type=MESH).start()

    def exchange(slot):
        for axis in AXES:
            for way in range(2):
                if axis == "gx":
                    src, dst = field[slot].at[:, nx if way == 0 else 1, pl.ds(0, ny), :], x_in.at[slot, way]
                elif axis == "gy":
                    src, dst = field[slot].at[:, pl.ds(1, nx), ny - 1 if way == 0 else 0, :], y_in.at[slot, way]
                else:
                    src, dst = z_out.at[slot, 0, way], z_in.at[slot, way]
                send(src, dst, slot, slot if axis == "gz" else 2 + slot, {axis: peers[axis][way]})

    def deep_exchange(slot):
        f = field[slot]
        for way in range(2):
            send(f.at[:, nx if way == 0 else 1, pl.ds(0, ny), :], x_near.at[way, :, pl.ds(PAD, ny), :], 2, 6, {"gx": peers["gx"][way]})
            send(f.at[:, pl.ds(1, nx), ny - 1 if way == 0 else 0, :], y_near.at[way, :, pl.ds(PAD, nx), :], 2, 6, {"gy": peers["gy"][way]})
        for way in range(2):
            send(z_out.at[slot, 0, way], z_near.at[way, pl.ds(PAD, ny), :], 2, 4, {"gz": peers["gz"][way]})
            send(z_out.at[slot, 1, way], z_far.at[way], 2, 4, {"gz": peers["gz"][way]})
            for other in range(2):
                row = pl.ds(ny - 1 if way == 0 else 0, 1)
                send(z_out.at[slot, 0, other], xz_in.at[way, other], 2, 4, {"gx": peers["gx"][way], "gz": peers["gz"][other]})
                send(z_out.at[slot, 0, other, row, :], yz_in.at[way, other, pl.ds(0, 1), :], 3, 5,
                     {"gy": peers["gy"][way], "gz": peers["gz"][other]})
                row = pl.ds(ny - 1 if other == 0 else 0, 1)
                send(f.at[:, nx if way == 0 else 1, row, :], xy_in.at[way, other, :, pl.ds(0, 1), :], 3, 5,
                     {"gx": peers["gx"][way], "gy": peers["gy"][other]})
        for way in range(2):
            send(f.at[:, nx - 1 if way == 0 else 2, pl.ds(0, ny), :], x_far.at[way], 2, 6, {"gx": peers["gx"][way]})
            send(f.at[:, pl.ds(1, nx), ny - 2 if way == 0 else 1, :], y_far.at[way], 2, 6, {"gy": peers["gy"][way]})

    def coefficients(kind):
        whole, lines = ((weight, weight_y), (rhs, rhs_y))[kind]
        for way in range(2):
            send(whole.at[:, nx - 1 if way == 0 else 0], x_coef.at[kind, way], 4, 7, {"gx": peers["gx"][way]})
            send(lines.at[0, 1 - way], y_coef.at[kind, way], 4, 7, {"gy": peers["gy"][way]})
            send(z_coef.at[kind, way], z_coef_in.at[kind, way], 4, 7, {"gz": peers["gz"][way]})

    def pack(skew, faces, first, final):
        return jnp.where(behind == skew, final, faces[0]), jnp.where(lane == skew, first, faces[1])

    def rotate_field(trip, faces):
        wait_planes(load_sem.at[trip], halves * STEP)
        for j in range(STEP):
            x = trip * STEP + j
            turned = [pltpu.roll(flat[1][half, plane_at(x), :], base + x, 1) for half in range(halves)]
            for half in range(halves):
                flat[0][half, plane_at(x), :] = turned[half]
            faces = pack(base + x, faces, turned[0], turned[last])
        return faces

    z_out[0, 0, 0], z_out[0, 0, 1] = lax.fori_loop(0, trips, rotate_field, (nothing, nothing))
    pl.semaphore_wait(barrier, 2 * len(AXES))
    exchange(0)

    def second(skew):
        return ahead == skew, behind_two == skew

    wait_planes(load_sem.at[trips], halves * nx)

    def rotate_weight(trip, faces):
        for j in range(STEP):
            x = trip * STEP + j
            turned = [WEIGHT / (6.0 + pltpu.roll(weight[half, x], base + x, 1)) for half in range(halves)]
            for half in range(halves):
                weight[half, x] = turned[half]
            next_low, next_high = second(base + x)
            faces = pack(base + x, faces[:2], turned[0], turned[last]) + (
                jnp.where(next_high, turned[last], faces[2]), jnp.where(next_low, turned[0], faces[3]))
        return faces

    z_coef[0, 0], z_coef[0, 1], inner_high, inner_low = lax.fori_loop(0, trips, rotate_weight, (nothing,) * 4)
    z_coef[2, 0], z_coef[2, 1] = inner_high, inner_low

    def lines_of(values, lines, inner):
        by_row = values.reshape(halves, nx * ny, LANES)
        for side in range(2):
            row = ny - 1 - inner if side else inner
            for half in range(halves):
                for x in range(0, nx, 8):
                    lines[inner, side, half, pl.ds(x, 8)] = by_row[half, pl.ds(x * ny + row, 8, stride=ny), :]

    lines_of(weight, weight_y, 0)
    wait_planes(load_sem.at[trips + 1], halves * nx)

    def rotate_rhs(trip, faces):
        for j in range(STEP):
            x = trip * STEP + j
            turned = [pltpu.roll(rhs[half, x], base + x, 1) for half in range(halves)]
            for half in range(halves):
                rhs[half, x] = turned[half]
            faces = pack(base + x, faces, turned[0], turned[last])
        return faces

    z_coef[1, 0], z_coef[1, 1] = lax.fori_loop(0, trips, rotate_rhs, (nothing, nothing))

    def sweep_inside(old, new):
        @pl.loop(0, trips)
        def _(trip):
            for j in range(STEP):
                x = trip * STEP + j
                here = [flat[old][half, plane_at(x), :] for half in range(halves)]
                at_first, at_last = lane == base + x, behind == base + x
                for half in range(halves):
                    after = jnp.where(at_first, here[half + 1] if half < last else 0.0, here[half]) + flat[old][half, plane_at(x + 1), :]
                    before = jnp.where(at_last, here[half - 1] if half > 0 else 0.0, here[half]) + flat[old][half, plane_at(x - 1), :]
                    beside = flat[old][half, plane_at(x, -1), :] + flat[old][half, plane_at(x, 1), :] + rhs[half, x]
                    beside = beside + (pltpu.roll(after, LANES - 1, 1) + pltpu.roll(before, 1, 1))
                    flat[new][half, plane_at(x), :] = KEEP * here[half] + weight[half, x] * beside

    for sweep in range(SWEEPS - 2):
        old, new = sweep % 2, (sweep + 1) % 2
        if sweep == 1:
            lines_of(weight, weight_y, 1)
            lines_of(rhs, rhs_y, 0)
            coefficients(0)
            coefficients(1)
        sweep_inside(old, new)
        deep = sweep == SWEEPS - 3

        wait_planes(recv_sem.at[old], 2)
        add_low = z_coef[0, 1] * pltpu.roll(z_in[old, 0], 1, 1)
        add_high = z_coef[0, 0] * pltpu.roll(z_in[old, 1], LANES - 1, 1)

        def finish(trip, faces):
            for j in range(STEP):
                x = trip * STEP + j
                at_first, at_last = lane == base + x, behind == base + x
                values = [flat[new][half, plane_at(x), :] for half in range(halves)]
                values[0] = values[0] + jnp.where(at_first, add_low, 0.0)
                values[last] = values[last] + jnp.where(at_last, add_high, 0.0)
                for half in range(halves):
                    flat[new][half, plane_at(x), :] = values[half]
                packed = pack(base + x, faces[:2], values[0], values[last])
                if deep:
                    next_low, next_high = second(base + x)
                    packed += (jnp.where(next_high, values[last], faces[2]), jnp.where(next_low, values[0], faces[3]))
                faces = packed
            return faces

        faces = list(lax.fori_loop(0, trips, finish, (nothing,) * (4 if deep else 2)))
        wait_planes(recv_sem.at[2 + old], 2 * (face + layer_planes))
        wait_planes(send_sem.at[old], 2 * (face + layer_planes) + 2)

        columns = [(behind, last, tall_last), (lane, 0, tall_first), (behind_two, last, tall_last_but_one), (ahead, 0, tall_second)]
        for way, turn in sides:
            x = (0, nx - 1)[way]
            late = [weight[half, x] * pltpu.roll(x_in[old, way, half], turn, 1) for half in range(halves)]
            for half in range(halves):
                flat[new][half, plane_at(x), :] += late[half]
            for i, (place, half, _) in enumerate(columns[:len(faces)]):
                faces[i] = faces[i] + jnp.where(place == base + x, late[half], 0.0)
        for i, packed in enumerate(faces):
            z_out[new, i // 2, i % 2] = packed
        for way, _ in sides:
            y = (0, ny - 1)[way]
            late = [weight_y[0, way, half] * y_in[old, way, half] for half in range(halves)]
            for half in range(halves):
                for x in range(0, nx, 8):
                    flat[new][half, row_at(x, y), :] += late[half][x:x + 8]
            for i, (_, half, mask) in enumerate(columns[:len(faces)]):
                z_out[new, i // 2, i % 2, pl.ds(y, 1)] += jnp.sum(jnp.where(mask, late[half], 0.0), axis=0, keepdims=True)
        if deep:
            deep_exchange(new)
        else:
            exchange(new)

    sweep_inside(0, 1)
    sweep_inside(1, 2)
    wait_planes(send_sem.at[4], 4 * (face + layer_planes) + 4)
    wait_planes(recv_sem.at[7], 4 * (face + layer_planes) + 4)
    wait_planes(recv_sem.at[4], 8)
    wait_lines(recv_sem.at[5], 4 * halves + 4)

    outside = (lax.rem(base + LANES - 1, LANES), lax.rem(base + nx, LANES))

    def along_plane(buf, skew, below, above, more_after=(0.0,) * halves, more_before=(0.0,) * halves):
        sums = []
        here = [buf[half, pl.ds(PAD, ny)] for half in range(halves)]
        for half in range(halves):
            after = jnp.where(lane == skew, here[half + 1] if half < last else above, here[half]) + more_after[half]
            before = jnp.where(behind == skew, here[half - 1] if half > 0 else below, here[half]) + more_before[half]
            sums.append(
                (buf[half, pl.ds(PAD - 1, ny)] + buf[half, pl.ds(PAD + 1, ny)])
                + (pltpu.roll(after, LANES - 1, 1) + pltpu.roll(before, 1, 1)))
        return sums

    def along_lines(buf, below, above):
        sums = []
        here = [buf[half, pl.ds(PAD, nx)] for half in range(halves)]
        for half in range(halves):
            after = jnp.where(tall_first, here[half + 1] if half < last else above, here[half]) + buf[half, pl.ds(PAD + 1, nx)]
            before = jnp.where(tall_last, here[half - 1] if half > 0 else below, here[half]) + buf[half, pl.ds(PAD - 1, nx)]
            sums.append(pltpu.roll(after, LANES - 1, 1) + pltpu.roll(before, 1, 1))
        return sums

    def along_columns(buf, here):
        return (buf[pl.ds(PAD - 1, ny)] + buf[pl.ds(PAD + 1, ny)]) + (pltpu.roll(here, LANES - 1, 1) + pltpu.roll(here, 1, 1))

    for way in range(2):
        for other in range(2):
            z_near[other, pl.ds((PAD - 1, PAD + ny)[way], 1)] = yz_in[way, other, pl.ds(0, 1)]
    z_total, z_inner = [], []
    for way, turn in sides:
        back = LANES - turn
        place = (behind, lane)[way]
        layer = z_near[way, pl.ds(PAD, ny)]
        full = jnp.where(place == outside[0], xz_in[0, way], jnp.where(place == outside[1], xz_in[1, way], layer))
        beyond = along_columns(z_near.at[way], full) + z_coef_in[1, way]
        beyond = beyond + (pltpu.roll(z_far[way], turn, 1) + pltpu.roll(z_out[0, 0, 1 - way], back, 1))
        ring = pltpu.roll(KEEP * layer + z_coef_in[0, way] * beyond, turn, 1)
        late = z_coef[0, 1 - way] * pltpu.roll(layer, turn, 1)
        z_add[way, pl.ds(PAD, ny)] = late
        z_total.append(z_coef[0, 1 - way] * (ring + along_columns(z_add.at[way], late)) + KEEP * late)
        z_inner.append(z_coef[2, 1 - way] * pltpu.roll(late, turn, 1))

    def store(x, first, turn):
        eight = slice(first, first + 8)
        skew = base + x
        values = [flat[2][half, pl.ds(pl.multiple_of((x + 1) * rows, 8) + first, 8), :] for half in range(halves)]
        values[0] = values[0] + jnp.where(
            lane[eight] == skew, z_total[0][eight], jnp.where(ahead[eight] == skew, z_inner[0][eight], 0.0))
        values[last] = values[last] + jnp.where(
            behind[eight] == skew, z_total[1][eight], jnp.where(behind_two[eight] == skew, z_inner[1][eight], 0.0))
        for half in range(halves):
            out[x, eight, half * LANES:(half + 1) * LANES] = pltpu.roll(values[half], turn, 1)

    middle = range(8, ny - 8, 8)

    @pl.loop(0, (nx - 4) // INNER)
    def _(trip):
        for j in range(INNER):
            x = trip * INNER + j + 2
            for first in middle:
                store(x, first, LANES - base - x)

    wait_planes(send_sem.at[2], 4 * (face + layer_planes) + 8)
    wait_lines(send_sem.at[3], 4 * halves + 4)
    wait_planes(recv_sem.at[6], 4 * (face + layer_planes))
    for way in range(2):
        for other in range(2):
            for half in range(halves):
                line = xy_in[way, other, half, pl.ds(0, 1)]
                x_near[way, half, pl.ds((PAD - 1, PAD + ny)[other], 1)] = line
                y_near[other, half, pl.ds((PAD - 1, PAD + nx)[way], 1)] = line
    for way, turn in sides:
        back = LANES - turn
        edge_x, edge_y = (0, nx - 1)[way], (0, ny - 1)[way]
        inner_x, inner_y = (1, nx - 2)[way], (1, ny - 2)[way]

        beyond = [x_far[way, half] for half in range(halves)]
        own = [flat[0][half, plane_at(edge_x), :] for half in range(halves)]
        ring = along_plane(
            x_near.at[way], outside[way], xz_in[way, 0], xz_in[way, 1], *((own, beyond) if way == 0 else (beyond, own)))
        for half in range(halves):
            layer = x_near[way, half, pl.ds(PAD, ny)]
            ring[half] = pltpu.roll(KEEP * layer + x_coef[0, way, half] * (ring[half] + x_coef[1, way, half]), turn, 1)
            x_add[way, half, pl.ds(PAD, ny)] = weight[half, edge_x] * pltpu.roll(layer, turn, 1)
        spread = along_plane(x_add.at[way], base + edge_x, 0.0, 0.0)
        for half in range(halves):
            late = x_add[way, half, pl.ds(PAD, ny)]
            flat[2][half, plane_at(edge_x), :] += weight[half, edge_x] * (ring[half] + spread[half]) + KEEP * late
            flat[2][half, plane_at(inner_x), :] += weight[half, inner_x] * pltpu.roll(late, turn, 1)

        ring = along_lines(y_near.at[way], yz_in[way, 0, pl.ds(0, 1)], yz_in[way, 1, pl.ds(0, 1)])
        for half in range(halves):
            layer = y_near[way, half, pl.ds(PAD, nx)]
            own = jnp.concatenate([flat[0][half, row_at(x, edge_y), :] for x in range(0, nx, 8)], axis=0)
            beyond = ring[half] + y_coef[1, way, half] + (y_far[way, half] + own)
            ring[half] = KEEP * layer + y_coef[0, way, half] * beyond
            y_add[way, half, pl.ds(PAD, nx)] = weight_y[0, way, half] * layer
        spread = along_lines(y_add.at[way], 0.0, 0.0)
        for half in range(halves):
            late = y_add[way, half, pl.ds(PAD, nx)]
            outer = weight_y[0, way, half] * (ring[half] + spread[half]) + KEEP * late
            inner = weight_y[1, way, half] * late
            for x in range(0, nx, 8):
                flat[2][half, row_at(x, edge_y), :] += outer[x:x + 8]
                flat[2][half, row_at(x, inner_y), :] += inner[x:x + 8]

    for x in (0, 1, nx - 2, nx - 1):
        for first in middle:
            store(x, first, LANES - base - x if x else lax.rem(LANES - base, LANES))

    @pl.loop(0, nx // OUTER)
    def _(trip):
        for j in range(OUTER):
            x = trip * OUTER + j
            for first in (0, ny - 8):
                store(x, first, LANES - base - x if j else lax.rem(LANES - base - x, LANES))


def relax(initial, right_side, shift_field):
    nx, ny, nz = initial.shape
    halves = nz // LANES
    plane, padded = (ny, LANES), (ny + 2 * PAD, LANES)
    layer = (nx, LANES)
    field = (halves, nx + 2, ny + PAD, LANES)
    shapes = [
        field, field, field, (halves, nx) + plane, (halves, nx) + plane, (2, 2, halves) + layer, (1, 2, halves) + layer,
        (3, 2) + plane, (2, 2, 2) + plane,
        (2, 2, halves) + plane, (2, 2, halves) + layer, (2, 2) + plane,
        (2, halves) + padded, (2, halves) + plane, (2, halves, nx + 2 * PAD, LANES), (2, halves) + layer, (2,) + padded, (2,) + plane,
        (2, 2, halves, PAD, LANES), (2, 2) + plane, (2, 2, PAD, LANES),
        (2, 2, halves) + plane, (2, 2, halves) + layer, (2, 2) + plane,
        (2, halves) + padded, (2, halves, nx + 2 * PAD, LANES), (2,) + padded,
    ]
    dma = pltpu.SemaphoreType.DMA
    return pl.pallas_call(
        kernel,
        out_shape=jax.ShapeDtypeStruct(initial.shape, jnp.float32),
        in_specs=[pl.BlockSpec(memory_space=pltpu.HBM)] * 3,
        out_specs=pl.BlockSpec(memory_space=pltpu.VMEM),
        scratch_shapes=[pltpu.VMEM(shape, jnp.float32) for shape in shapes]
        + [dma((nx // STEP + 2,)), dma((5,)), dma((8,))],
        compiler_params=pltpu.CompilerParams(collective_id=0, has_side_effects=True, vmem_limit_bytes=32 * 2**20),
    )(*(pltpu.with_memory_space_constraint(a, pltpu.HBM) for a in (initial, right_side, shift_field)))


def solution(mesh):
    return jax.shard_map(
        relax,
        mesh=mesh,
        in_specs=(P(*AXES), P(*AXES), P(*AXES)),
        out_specs=P(*AXES),
        check_vma=False,
    )
```

time: 25.1 us -> 23.5 us (0.936)
  Pallas kernels: 23.7 us -> 22.1 us
    pallas_call x1, Pallas kernels: 23.7 us -> 22.1 us  [relax(): pl.pallas_call(kernel, out_shape=jax.ShapeDtypeStruct(initial.shape, jnp....]
where the time goes in v4:
time: 23.5 us; the launch traced here: 23.4 us
  Pallas kernels  22.1 us (94%)
  local copies, waits for them, and re-layouts  1.32 us (6%)
    pallas_call x1, Pallas kernels, relax(): pl.pallas_call(kernel, out_shape=jax.ShapeDtypeStruct(initial.shape, jnp....  22.1 us
    unnamed x1, local copies, waits for them, and re-layouts  1.32 us

profile of v4, /device:TPU:1, one launch (start us, length us, event | category | flops | bytes accessed | tf_op | source)
XLA Modules:
  0.0 23.4 jit_solution(12184178927662245016)
XLA Ops:
  0.0 22.1 %shard_map.37 = f32[64,32,256]{2,1,0:T(8,128)S(1)} custom-call(f32[64,32,256]{2,1,0:T(8,128)} %init_hbm.1, f32[64,32,256]{2,1,0:T(8,128)} %rhs_hbm.1, f32[64,32,256]{2,1,0:T(8,128)} %shift_hbm.1), custom_call_target="tpu_custom_call" | custom-call | tf_op jit(solution)/shard_map/pallas_call | solution.py:425
  22.1 1.3 %copy.5 = f32[64,32,256]{2,1,0:T(8,128)} copy(f32[64,32,256]{2,1,0:T(8,128)S(1)} %shard_map.37) | data formatting | bytes 4194304

commit v5 on v4

--- a/solution.py
+++ b/solution.py
@@ -34,6 +34,11 @@
     base = lax.rem(lax.axis_index("gx"), 2) * nx
     sides = ((0, 1), (1, LANES - 1))
 
+    barrier = pltpu.get_barrier_semaphore()
+    for axis in AXES:
+        for peer in peers[axis]:
+            pl.semaphore_signal(barrier, inc=1, device_id={axis: peer}, device_id_type=MESH)
+
     all_planes = rhs.reshape(halves * nx, ny, LANES)
     face, layer_planes = halves, halves * nx // ny
 
@@ -67,11 +72,6 @@
     for group in loads:
         for copy in group:
             copy.start()
-    barrier = pltpu.get_barrier_semaphore()
-    for axis in AXES:
-        for peer in peers[axis]:
-            pl.semaphore_signal(barrier, inc=1, device_id={axis: peer}, device_id_type=MESH)
-
     lane = lax.broadcasted_iota(jnp.int32, (ny, LANES), 1)
     behind = jnp.where(lane == LANES - 1, 0, lane + 1)
     behind_two = jnp.where(behind == LANES - 1, 0, behind + 1)
@@ -104,11 +104,12 @@
     edge = jnp.zeros((PAD, LANES), jnp.float32)
     for way in range(2):
         for half in range(halves):
-            for ref, size in ((x_add.at[way, half], ny), (y_add.at[way, half], nx)):
+            for ref, size in ((x_add.at[way, half], ny), (y_add.at[way, half], nx), (x_near.at[way, half], ny), (y_near.at[way, half], nx)):
                 ref[pl.ds(0, PAD)] = edge
                 ref[pl.ds(PAD + size, PAD)] = edge
-        z_add[way, pl.ds(0, PAD)] = edge
-        z_add[way, pl.ds(PAD + ny, PAD)] = edge
+        for ref in (z_add.at[way], z_near.at[way]):
+            ref[pl.ds(0, PAD)] = edge
+            ref[pl.ds(PAD + ny, PAD)] = edge
 
     def send(src, dst, sent, received, target):
         pltpu.make_async_remote_copy(
@@ -135,7 +136,7 @@
             send(z_out.at[slot, 1, way], z_far.at[way], 2, 4, {"gz": peers["gz"][way]})
             for other in range(2):
                 row = pl.ds(ny - 1 if way == 0 else 0, 1)
-                send(z_out.at[slot, 0, other], xz_in.at[way, other], 2, 4, {"gx": peers["gx"][way], "gz": peers["gz"][other]})
+                send(z_out.at[slot, 0, other], xz_in.at[way, other], 2, 8, {"gx": peers["gx"][way], "gz": peers["gz"][other]})
                 send(z_out.at[slot, 0, other, row, :], yz_in.at[way, other, pl.ds(0, 1), :], 3, 5,
                      {"gy": peers["gy"][way], "gz": peers["gz"][other]})
                 row = pl.ds(ny - 1 if other == 0 else 0, 1)
@@ -227,6 +228,7 @@
     for sweep in range(SWEEPS - 2):
         old, new = sweep % 2, (sweep + 1) % 2
         if sweep == 1:
+            wait_planes(send_sem.at[0], 2 * (face + layer_planes) + 2)
             lines_of(weight, weight_y, 1)
             lines_of(rhs, rhs_y, 0)
             coefficients(0)
@@ -256,7 +258,6 @@
 
         faces = list(lax.fori_loop(0, trips, finish, (nothing,) * (4 if deep else 2)))
         wait_planes(recv_sem.at[2 + old], 2 * (face + layer_planes))
-        wait_planes(send_sem.at[old], 2 * (face + layer_planes) + 2)
 
         columns = [(behind, last, tall_last), (lane, 0, tall_first), (behind_two, last, tall_last_but_one), (ahead, 0, tall_second)]
         for way, turn in sides:
@@ -281,12 +282,11 @@
         else:
             exchange(new)
 
+    wait_planes(send_sem.at[1], 2 * (face + layer_planes) + 2)
     sweep_inside(0, 1)
     sweep_inside(1, 2)
-    wait_planes(send_sem.at[4], 4 * (face + layer_planes) + 4)
     wait_planes(recv_sem.at[7], 4 * (face + layer_planes) + 4)
-    wait_planes(recv_sem.at[4], 8)
-    wait_lines(recv_sem.at[5], 4 * halves + 4)
+    wait_planes(recv_sem.at[4], 4)
 
     outside = (lax.rem(base + LANES - 1, LANES), lax.rem(base + nx, LANES))
 
@@ -313,16 +313,11 @@
     def along_columns(buf, here):
         return (buf[pl.ds(PAD - 1, ny)] + buf[pl.ds(PAD + 1, ny)]) + (pltpu.roll(here, LANES - 1, 1) + pltpu.roll(here, 1, 1))
 
-    for way in range(2):
-        for other in range(2):
-            z_near[other, pl.ds((PAD - 1, PAD + ny)[way], 1)] = yz_in[way, other, pl.ds(0, 1)]
     z_total, z_inner = [], []
     for way, turn in sides:
         back = LANES - turn
-        place = (behind, lane)[way]
         layer = z_near[way, pl.ds(PAD, ny)]
-        full = jnp.where(place == outside[0], xz_in[0, way], jnp.where(place == outside[1], xz_in[1, way], layer))
-        beyond = along_columns(z_near.at[way], full) + z_coef_in[1, way]
+        beyond = along_columns(z_near.at[way], layer) + z_coef_in[1, way]
         beyond = beyond + (pltpu.roll(z_far[way], turn, 1) + pltpu.roll(z_out[0, 0, 1 - way], back, 1))
         ring = pltpu.roll(KEEP * layer + z_coef_in[0, way] * beyond, turn, 1)
         late = z_coef[0, 1 - way] * pltpu.roll(layer, turn, 1)
@@ -350,15 +345,7 @@
             for first in middle:
                 store(x, first, LANES - base - x)
 
-    wait_planes(send_sem.at[2], 4 * (face + layer_planes) + 8)
-    wait_lines(send_sem.at[3], 4 * halves + 4)
     wait_planes(recv_sem.at[6], 4 * (face + layer_planes))
-    for way in range(2):
-        for other in range(2):
-            for half in range(halves):
-                line = xy_in[way, other, half, pl.ds(0, 1)]
-                x_near[way, half, pl.ds((PAD - 1, PAD + ny)[other], 1)] = line
-                y_near[other, half, pl.ds((PAD - 1, PAD + nx)[way], 1)] = line
     for way, turn in sides:
         back = LANES - turn
         edge_x, edge_y = (0, nx - 1)[way], (0, ny - 1)[way]
@@ -367,7 +354,7 @@
         beyond = [x_far[way, half] for half in range(halves)]
         own = [flat[0][half, plane_at(edge_x), :] for half in range(halves)]
         ring = along_plane(
-            x_near.at[way], outside[way], xz_in[way, 0], xz_in[way, 1], *((own, beyond) if way == 0 else (beyond, own)))
+            x_near.at[way], outside[way], 0.0, 0.0, *((own, beyond) if way == 0 else (beyond, own)))
         for half in range(halves):
             layer = x_near[way, half, pl.ds(PAD, ny)]
             ring[half] = pltpu.roll(KEEP * layer + x_coef[0, way, half] * (ring[half] + x_coef[1, way, half]), turn, 1)
@@ -378,7 +365,7 @@
             flat[2][half, plane_at(edge_x), :] += weight[half, edge_x] * (ring[half] + spread[half]) + KEEP * late
             flat[2][half, plane_at(inner_x), :] += weight[half, inner_x] * pltpu.roll(late, turn, 1)
 
-        ring = along_lines(y_near.at[way], yz_in[way, 0, pl.ds(0, 1)], yz_in[way, 1, pl.ds(0, 1)])
+        ring = along_lines(y_near.at[way], 0.0, 0.0)
         for half in range(halves):
             layer = y_near[way, half, pl.ds(PAD, nx)]
             own = jnp.concatenate([flat[0][half, row_at(x, edge_y), :] for x in range(0, nx, 8)], axis=0)
@@ -394,6 +381,36 @@
                 flat[2][half, row_at(x, edge_y), :] += outer[x:x + 8]
                 flat[2][half, row_at(x, inner_y), :] += inner[x:x + 8]
 
+    wait_planes(recv_sem.at[8], 4)
+    wait_lines(recv_sem.at[5], 4 * halves + 4)
+    row_of = lax.broadcasted_iota(jnp.int32, (ny, LANES), 0)
+    for way, turn in sides:
+        edge_x, edge_y = (0, nx - 1)[way], (0, ny - 1)[way]
+        for other, other_turn in sides:
+            half = (0, last)[other]
+            place = (behind, lane)[other]
+
+            y = (0, ny - 1)[other]
+            for each in range(halves):
+                line = xy_in[way, other, each, pl.ds(0, 1)]
+                through = pltpu.roll(x_coef[0, way, each, pl.ds(y, 1)] * line, turn, 1)
+                through = through + y_coef[0, other, each, pl.ds(edge_x, 1)] * pltpu.roll(line, turn, 1)
+                flat[2][each, pl.ds((edge_x + 1) * rows + y, 1), :] += weight_y[0, other, each, pl.ds(edge_x, 1)] * through
+
+            only = jnp.where(place == outside[way], xz_in[way, other], 0.0)
+            through = pltpu.roll(x_coef[0, way, half] * pltpu.roll(only, other_turn, 1), turn, 1)
+            flat[2][half, plane_at(edge_x), :] += weight[half, edge_x] * through
+            through = pltpu.roll(z_coef_in[0, other] * pltpu.roll(only, turn, 1), other_turn, 1)
+            z_total[other] = z_total[other] + z_coef[0, 1 - other] * through
+
+            line = yz_in[way, other, pl.ds(0, 1)]
+            through = pltpu.roll(jnp.where(row_of == edge_y, z_coef_in[0, other] * line, 0.0), other_turn, 1)
+            z_total[other] = z_total[other] + z_coef[0, 1 - other] * through
+            only = jnp.where((tall_last, tall_first)[other], line, 0.0)
+            through = weight_y[0, way, half] * (y_coef[0, way, half] * pltpu.roll(only, other_turn, 1))
+            for x in range(0, nx, 8):
+                flat[2][half, row_at(x, edge_y), :] += through[x:x + 8]
+
     for x in (0, 1, nx - 2, nx - 1):
         for first in middle:
             store(x, first, LANES - base - x if x else lax.rem(LANES - base, LANES))
@@ -404,6 +421,10 @@
             x = trip * OUTER + j
             for first in (0, ny - 8):
                 store(x, first, LANES - base - x if j else lax.rem(LANES - base - x, LANES))
+
+    wait_planes(send_sem.at[4], 4 * (face + layer_planes) + 4)
+    wait_planes(send_sem.at[2], 4 * (face + layer_planes) + 8)
+    wait_lines(send_sem.at[3], 4 * halves + 4)
 
 
 def relax(initial, right_side, shift_field):
@@ -428,7 +449,7 @@
         in_specs=[pl.BlockSpec(memory_space=pltpu.HBM)] * 3,
         out_specs=pl.BlockSpec(memory_space=pltpu.VMEM),
         scratch_shapes=[pltpu.VMEM(shape, jnp.float32) for shape in shapes]
-        + [dma((nx // STEP + 2,)), dma((5,)), dma((8,))],
+        + [dma((nx // STEP + 2,)), dma((5,)), dma((9,))],
         compiler_params=pltpu.CompilerParams(collective_id=0, has_side_effects=True, vmem_limit_bytes=32 * 2**20),
     )(*(pltpu.with_memory_space_constraint(a, pltpu.HBM) for a in (initial, right_side, shift_field)))
 

time: 23.5 us -> 22.7 us (0.966)
  Pallas kernels: 22.1 us -> 21.3 us
    pallas_call x1, Pallas kernels: 22.1 us -> 21.3 us  [relax(): pl.pallas_call(kernel, out_shape=jax.ShapeDtypeStruct(initial.shape, jnp....]
where the time goes in v5:
time: 22.7 us; the launch traced here: 22.6 us
  Pallas kernels  21.3 us (94%)
  local copies, waits for them, and re-layouts  1.32 us (6%)
    pallas_call x1, Pallas kernels, relax(): pl.pallas_call(kernel, out_shape=jax.ShapeDtypeStruct(initial.shape, jnp....  21.3 us
    unnamed x1, local copies, waits for them, and re-layouts  1.32 us

profile of v5, /device:TPU:1, one launch (start us, length us, event | category | flops | bytes accessed | tf_op | source)
XLA Modules:
  0.0 22.6 jit_solution(15644516616434298539)
XLA Ops:
  0.0 21.3 %shard_map.37 = f32[64,32,256]{2,1,0:T(8,128)S(1)} custom-call(f32[64,32,256]{2,1,0:T(8,128)} %init_hbm.1, f32[64,32,256]{2,1,0:T(8,128)} %rhs_hbm.1, f32[64,32,256]{2,1,0:T(8,128)} %shift_hbm.1), custom_call_target="tpu_custom_call" | custom-call | tf_op jit(solution)/shard_map/pallas_call | solution.py:446
  21.3 1.3 %copy.5 = f32[64,32,256]{2,1,0:T(8,128)} copy(f32[64,32,256]{2,1,0:T(8,128)S(1)} %shard_map.37) | data formatting | bytes 4194304

commit v6 on v5

--- a/solution.py
+++ b/solution.py
@@ -13,7 +13,7 @@
 LANES = 128
 PAD = 8
 STEP = 16
-INNER, OUTER = 20, 32
+INNER, OUTER = 20, 64
 
 
 def kernel(
@@ -129,9 +129,6 @@
     def deep_exchange(slot):
         f = field[slot]
         for way in range(2):
-            send(f.at[:, nx if way == 0 else 1, pl.ds(0, ny), :], x_near.at[way, :, pl.ds(PAD, ny), :], 2, 6, {"gx": peers["gx"][way]})
-            send(f.at[:, pl.ds(1, nx), ny - 1 if way == 0 else 0, :], y_near.at[way, :, pl.ds(PAD, nx), :], 2, 6, {"gy": peers["gy"][way]})
-        for way in range(2):
             send(z_out.at[slot, 0, way], z_near.at[way, pl.ds(PAD, ny), :], 2, 4, {"gz": peers["gz"][way]})
             send(z_out.at[slot, 1, way], z_far.at[way], 2, 4, {"gz": peers["gz"][way]})
             for other in range(2):
@@ -142,6 +139,9 @@
                 row = pl.ds(ny - 1 if other == 0 else 0, 1)
                 send(f.at[:, nx if way == 0 else 1, row, :], xy_in.at[way, other, :, pl.ds(0, 1), :], 3, 5,
                      {"gx": peers["gx"][way], "gy": peers["gy"][other]})
+        for way in range(2):
+            send(f.at[:, nx if way == 0 else 1, pl.ds(0, ny), :], x_near.at[way, :, pl.ds(PAD, ny), :], 2, 6, {"gx": peers["gx"][way]})
+            send(f.at[:, pl.ds(1, nx), ny - 1 if way == 0 else 0, :], y_near.at[way, :, pl.ds(PAD, nx), :], 2, 6, {"gy": peers["gy"][way]})
         for way in range(2):
             send(f.at[:, nx - 1 if way == 0 else 2, pl.ds(0, ny), :], x_far.at[way], 2, 6, {"gx": peers["gx"][way]})
             send(f.at[:, pl.ds(1, nx), ny - 2 if way == 0 else 1, :], y_far.at[way], 2, 6, {"gy": peers["gy"][way]})
@@ -381,33 +381,36 @@
                 flat[2][half, row_at(x, edge_y), :] += outer[x:x + 8]
                 flat[2][half, row_at(x, inner_y), :] += inner[x:x + 8]
 
-    wait_planes(recv_sem.at[8], 4)
-    wait_lines(recv_sem.at[5], 4 * halves + 4)
-    row_of = lax.broadcasted_iota(jnp.int32, (ny, LANES), 0)
+    xy_factor, xz_factor, yz_factor = {}, {}, {}
     for way, turn in sides:
         edge_x, edge_y = (0, nx - 1)[way], (0, ny - 1)[way]
         for other, other_turn in sides:
             half = (0, last)[other]
-            place = (behind, lane)[other]
-
             y = (0, ny - 1)[other]
             for each in range(halves):
-                line = xy_in[way, other, each, pl.ds(0, 1)]
-                through = pltpu.roll(x_coef[0, way, each, pl.ds(y, 1)] * line, turn, 1)
-                through = through + y_coef[0, other, each, pl.ds(edge_x, 1)] * pltpu.roll(line, turn, 1)
-                flat[2][each, pl.ds((edge_x + 1) * rows + y, 1), :] += weight_y[0, other, each, pl.ds(edge_x, 1)] * through
-
-            only = jnp.where(place == outside[way], xz_in[way, other], 0.0)
-            through = pltpu.roll(x_coef[0, way, half] * pltpu.roll(only, other_turn, 1), turn, 1)
-            flat[2][half, plane_at(edge_x), :] += weight[half, edge_x] * through
-            through = pltpu.roll(z_coef_in[0, other] * pltpu.roll(only, turn, 1), other_turn, 1)
-            z_total[other] = z_total[other] + z_coef[0, 1 - other] * through
-
-            line = yz_in[way, other, pl.ds(0, 1)]
-            through = pltpu.roll(jnp.where(row_of == edge_y, z_coef_in[0, other] * line, 0.0), other_turn, 1)
-            z_total[other] = z_total[other] + z_coef[0, 1 - other] * through
-            only = jnp.where((tall_last, tall_first)[other], line, 0.0)
-            through = weight_y[0, way, half] * (y_coef[0, way, half] * pltpu.roll(only, other_turn, 1))
+                through = pltpu.roll(x_coef[0, way, each, pl.ds(y, 1)], turn, 1) + y_coef[0, other, each, pl.ds(edge_x, 1)]
+                xy_factor[way, other, each] = weight_y[0, other, each, pl.ds(edge_x, 1)] * through
+            through = pltpu.roll(x_coef[0, way, half], turn, 1) + pltpu.roll(z_coef_in[0, other], other_turn, 1)
+            xz_factor[way, other] = weight[half, edge_x] * through
+            through = y_coef[0, way, half] + pltpu.roll(z_coef_in[0, other, pl.ds(edge_y, 1)], other_turn, 1)
+            yz_factor[way, other] = jnp.where(
+                (tall_first, tall_last)[other], weight_y[0, way, half] * through, 0.0)
+
+    wait_planes(recv_sem.at[8], 4)
+    wait_lines(recv_sem.at[5], 4 * halves + 4)
+    for way, turn in sides:
+        edge_x, edge_y = (0, nx - 1)[way], (0, ny - 1)[way]
+        for other, other_turn in sides:
+            half = (0, last)[other]
+            y = (0, ny - 1)[other]
+            for each in range(halves):
+                line = pltpu.roll(xy_in[way, other, each, pl.ds(0, 1)], turn, 1)
+                flat[2][each, pl.ds((edge_x + 1) * rows + y, 1), :] += xy_factor[way, other, each] * line
+            column = pltpu.roll(xz_in[way, other], (turn + other_turn) % LANES, 1)
+            at_edge = (lane, behind)[other] == base + edge_x
+            flat[2][half, plane_at(edge_x), :] += jnp.where(at_edge, xz_factor[way, other] * column, 0.0)
+            line = pltpu.roll(yz_in[way, other, pl.ds(0, 1)], other_turn, 1)
+            through = yz_factor[way, other] * line
             for x in range(0, nx, 8):
                 flat[2][half, row_at(x, edge_y), :] += through[x:x + 8]
 

time: 22.7 us -> 22.2 us (0.978)
  Pallas kernels: 21.3 us -> 20.8 us
    pallas_call x1, Pallas kernels: 21.3 us -> 20.8 us  [relax(): pl.pallas_call(kernel, out_shape=jax.ShapeDtypeStruct(initial.shape, jnp....]
where the time goes in v6:
time: 22.2 us; the launch traced here: 22.1 us
  Pallas kernels  20.8 us (94%)
  local copies, waits for them, and re-layouts  1.32 us (6%)
    pallas_call x1, Pallas kernels, relax(): pl.pallas_call(kernel, out_shape=jax.ShapeDtypeStruct(initial.shape, jnp....  20.8 us
    unnamed x1, local copies, waits for them, and re-layouts  1.32 us

profile of v6, /device:TPU:1, one launch (start us, length us, event | category | flops | bytes accessed | tf_op | source)
XLA Modules:
  0.0 22.1 jit_solution(10567639372552510521)
XLA Ops:
  0.0 20.8 %shard_map.37 = f32[64,32,256]{2,1,0:T(8,128)S(1)} custom-call(f32[64,32,256]{2,1,0:T(8,128)} %init_hbm.1, f32[64,32,256]{2,1,0:T(8,128)} %rhs_hbm.1, f32[64,32,256]{2,1,0:T(8,128)} %shift_hbm.1), custom_call_target="tpu_custom_call" | custom-call | tf_op jit(solution)/shard_map/pallas_call | solution.py:449
  20.8 1.3 %copy.5 = f32[64,32,256]{2,1,0:T(8,128)} copy(f32[64,32,256]{2,1,0:T(8,128)S(1)} %shard_map.37) | data formatting | bytes 4194304
